TPU v7x, 32 devices: a whole 2x2x4 slice. The times are simulated.
32 devices in a mesh: fsdp: 8 (over z, x), dp: 4 (over y, core).
Axes of the slice: x: 2, y: 2, z: 4, core: 2. Of those that a mesh axis runs over, the one named last changes fastest.
Arguments:
- inputs: bfloat16 [32768, 768], P(('fsdp', 'dp')), may hold values from -6 to 6
- row_ids: int32 [32768], P(('fsdp', 'dp')), may hold values from 0 to 7, as said below
- ln_gains: bfloat16 [2, 768], P(None, 'fsdp'), may hold values from 0.099609375 to 1.8984375
- biases: bfloat16 [6, 768], P(None, 'fsdp'), may hold values from -3 to 3
- w_qkv: bfloat16 [768, 2304], P('fsdp'), may hold values from -0.21875 to 0.21875
- w_out: bfloat16 [768, 768], P('fsdp'), may hold values from -0.75 to 0.75
- w_up: bfloat16 [768, 3072], P('fsdp'), may hold values from -0.21875 to 0.21875
- bias_up: bfloat16 [3072], P('fsdp'), may hold values from -3 to 3
- w_down: bfloat16 [3072, 768], P('fsdp'), may hold values from -0.109375 to 0.109375
- cotangent: bfloat16 [32768, 768], P(('fsdp', 'dp')), may hold values from -6 to 6
Outputs:
- block_out: bfloat16 [32768, 768], P(('fsdp', 'dp'))
- d_inputs: float32 [32768, 768], P(('fsdp', 'dp'))
- g_ln_gains: float32 [2, 768], P(None, 'fsdp')
- g_biases: float32 [6, 768], P(None, 'fsdp')
- g_w_qkv: float32 [768, 2304], P('fsdp')
- g_w_out: float32 [768, 768], P('fsdp')
- g_w_up: float32 [768, 3072], P('fsdp')
- g_bias_up: float32 [3072], P('fsdp')
- g_w_down: float32 [3072, 768], P('fsdp')
Inputs may be any that keep to these rules, and one draw needn't show every extreme that they name: `row_ids`: on each device the 1024 tokens form rows of 128 or 256 consecutive tokens, the longer rows first, so that each row starts at a multiple of its own length; the value numbers a token's row on its device from 0 in order; some device holds only rows of 128.
All inputs are finite; a program needn't handle non-finite values.
Results may differ from a plain program's by a relative error of at most 0.011.
Values may be sent and summed in bfloat16 or wider, within the bound.
A program may use at most 256 MiB of HBM per device.

v0:
```python
import math

import jax
import jax.numpy as jnp
from jax import lax
from jax.sharding import PartitionSpec as P

HEADS = 12
HEAD = 64
BLOCK = 512


norm_eps = 1e-05


def layer_norm(values, gain, shift):
    center = values - jnp.mean(values, axis=-1, keepdims=True)
    spread = jnp.mean(center * center, axis=-1, keepdims=True)
    return center * lax.rsqrt(spread + norm_eps) * gain + shift


def gelu_tanh(values):
    inner = math.sqrt(2.0 / math.pi) * (values + 0.044715 * values * values * values)
    return 0.5 * values * (1.0 + jnp.tanh(inner))


def contract_rows(left, right):
    return lax.dot_general(
        left, right, (((0,), (0,)), ((), ())), preferred_element_type=jnp.float32
    )


def contract_cols(left, right):
    return lax.dot_general(
        left, right, (((1,), (1,)), ((), ())), preferred_element_type=jnp.float32
    )


def split_heads(values):
    return values.reshape(values.shape[0], HEADS, values.shape[1] // HEADS)


def block_scores(query, keys, query_rows, key_rows):
    raw_scores = jnp.einsum(
        "qhd,khd->hqk", split_heads(query), split_heads(keys), preferred_element_type=jnp.float32
    )
    raw_scores = raw_scores * (1.0 / math.sqrt(HEAD))
    same_row = (query_rows[:, None] == key_rows[None, :])[None]
    return jnp.where(same_row, raw_scores, -1000000000.0)


def attend_forward(query, keys, values, query_rows, key_rows):
    scores = block_scores(query, keys, query_rows, key_rows)
    row_max = jnp.max(scores, axis=-1, keepdims=True)
    exponent = jnp.exp(scores - row_max)
    row_sum = jnp.sum(exponent, axis=-1, keepdims=True)
    attn_probs = (exponent / row_sum).astype(jnp.bfloat16)
    result = jnp.einsum(
        "hqk,khd->qhd", attn_probs, split_heads(values), preferred_element_type=jnp.float32
    )
    return (result.reshape(query.shape[0], -1), (row_max + jnp.log(row_sum))[..., 0])


def attend_backward(query, keys, values, query_rows, key_rows, log_sums, grad_out):
    scores = block_scores(query, keys, query_rows, key_rows)
    attn_probs = jnp.exp(scores - log_sums[..., None])
    probs_low = attn_probs.astype(jnp.bfloat16)
    grad_heads = split_heads(grad_out)
    d_values = jnp.einsum("hqk,qhd->khd", probs_low, grad_heads, preferred_element_type=jnp.float32)
    d_probs = jnp.einsum(
        "qhd,khd->hqk", grad_heads, split_heads(values), preferred_element_type=jnp.float32
    )
    inner = jnp.sum(attn_probs * d_probs, axis=-1, keepdims=True)
    d_scores = (attn_probs * (d_probs - inner)).astype(jnp.bfloat16)
    scale = 1.0 / math.sqrt(HEAD)
    d_query = (
        jnp.einsum("hqk,khd->qhd", d_scores, split_heads(keys), preferred_element_type=jnp.float32)
        * scale
    )
    d_keys = (
        jnp.einsum("hqk,qhd->khd", d_scores, split_heads(query), preferred_element_type=jnp.float32)
        * scale
    )
    return (
        d_query.reshape(query.shape[0], -1),
        d_keys.reshape(keys.shape[0], -1),
        d_values.reshape(keys.shape[0], -1),
    )


def per_device(inputs, row_ids, ln_gains, biases, w_qkv, w_out, w_up, bias_up, w_down, cotangent):
    gathered = (
        lax.all_gather(ln_gains, "fsdp", axis=1, tiled=True),
        lax.all_gather(biases, "fsdp", axis=1, tiled=True),
        lax.all_gather(w_qkv, "fsdp", axis=0, tiled=True),
        lax.all_gather(w_out, "fsdp", axis=0, tiled=True),
        lax.all_gather(w_up, "fsdp", axis=0, tiled=True),
        lax.all_gather(bias_up, "fsdp", axis=0, tiled=True),
        lax.all_gather(w_down, "fsdp", axis=0, tiled=True),
    )
    gains = gathered[0].astype(jnp.float32)
    shifts = gathered[1].astype(jnp.float32)
    full_qkv, full_out, full_up, full_bias_up, full_down = (
        gathered[2],
        gathered[3],
        gathered[4],
        gathered[5],
        gathered[6],
    )
    width = full_out.shape[0]
    rows_n = inputs.shape[0]
    blocks_n = rows_n // BLOCK
    tokens_f = inputs.astype(jnp.float32)
    normed_f, norm_pull = jax.vjp(layer_norm, tokens_f, gains[0], shifts[0])
    normed = normed_f.astype(jnp.bfloat16)
    qkv_bias = jnp.concatenate([shifts[1], jnp.zeros_like(shifts[1]), shifts[2]])
    qkv = (jnp.dot(normed, full_qkv, preferred_element_type=jnp.float32) + qkv_bias).astype(
        jnp.bfloat16
    )
    query = qkv[:, :width]
    keys = qkv[:, width : 2 * width]
    values = qkv[:, 2 * width :]
    query_blocks = query.reshape(blocks_n, BLOCK, width)
    row_blocks = row_ids.reshape(blocks_n, BLOCK)

    def forward_block(entry):
        return attend_forward(entry[0], keys, values, entry[1], row_ids)

    mixed, log_sums = lax.map(forward_block, (query_blocks, row_blocks))
    mixed = mixed.reshape(rows_n, width).astype(jnp.bfloat16)
    middle = tokens_f + jnp.dot(mixed, full_out, preferred_element_type=jnp.float32) + shifts[3]
    normed_two_f, second_pull = jax.vjp(layer_norm, middle, gains[1], shifts[4])
    normed_two = normed_two_f.astype(jnp.bfloat16)
    upper = jnp.dot(normed_two, full_up, preferred_element_type=jnp.float32) + full_bias_up.astype(
        jnp.float32
    )
    hidden_f, gelu_pull = jax.vjp(gelu_tanh, upper)
    hidden = hidden_f.astype(jnp.bfloat16)
    block_out = (
        middle + jnp.dot(hidden, full_down, preferred_element_type=jnp.float32) + shifts[5]
    ).astype(jnp.bfloat16)
    again = (
        lax.all_gather(ln_gains, "fsdp", axis=1, tiled=True),
        lax.all_gather(biases, "fsdp", axis=1, tiled=True),
        lax.all_gather(w_qkv, "fsdp", axis=0, tiled=True),
        lax.all_gather(w_out, "fsdp", axis=0, tiled=True),
        lax.all_gather(w_up, "fsdp", axis=0, tiled=True),
        lax.all_gather(bias_up, "fsdp", axis=0, tiled=True),
        lax.all_gather(w_down, "fsdp", axis=0, tiled=True),
    )
    back_qkv, back_out, back_up, back_down = (again[2], again[3], again[4], again[6])
    grad_out = cotangent.astype(jnp.float32)
    grad_shift_down = jnp.sum(grad_out, axis=0)
    grad_down = contract_rows(hidden, cotangent)
    d_hidden = contract_cols(cotangent, back_down)
    d_up = gelu_pull(d_hidden)[0].astype(jnp.bfloat16)
    grad_up = contract_rows(normed_two, d_up)
    grad_bias_up = jnp.sum(d_up, axis=0, dtype=jnp.float32)
    d_normed_two = contract_cols(d_up, back_up)
    d_middle_norm, grad_gain_two, grad_shift_two = second_pull(d_normed_two)
    d_middle = grad_out + d_middle_norm
    grad_shift_out = jnp.sum(d_middle, axis=0)
    d_middle_low = d_middle.astype(jnp.bfloat16)
    grad_out_proj = contract_rows(mixed, d_middle_low)
    d_mixed = contract_cols(d_middle_low, back_out).astype(jnp.bfloat16)
    d_blocks = d_mixed.reshape(blocks_n, BLOCK, width)

    def backward_step(carry, entry):
        d_query, d_keys, d_values = attend_backward(
            entry[0], keys, values, entry[1], row_ids, entry[2], entry[3]
        )
        return ((carry[0] + d_keys, carry[1] + d_values), d_query)

    empty = jnp.zeros((rows_n, width), jnp.float32)
    (d_keys, d_values), d_query = lax.scan(
        backward_step, (empty, empty), (query_blocks, row_blocks, log_sums, d_blocks)
    )
    d_query = d_query.reshape(rows_n, width)
    d_qkv = jnp.concatenate([d_query, d_keys, d_values], axis=1).astype(jnp.bfloat16)
    grad_qkv = contract_rows(normed, d_qkv)
    grad_bias_query = jnp.sum(d_qkv[:, :width], axis=0, dtype=jnp.float32)
    grad_bias_value = jnp.sum(d_qkv[:, 2 * width :], axis=0, dtype=jnp.float32)
    d_normed = contract_cols(d_qkv, back_qkv)
    d_tokens_norm, grad_gain_one, grad_shift_one = norm_pull(d_normed)
    d_inputs = d_middle + d_tokens_norm
    grad_gains = jnp.stack([grad_gain_one, grad_gain_two])
    grad_shifts = jnp.stack(
        [
            grad_shift_one,
            grad_bias_query,
            grad_bias_value,
            grad_shift_out,
            grad_shift_two,
            grad_shift_down,
        ]
    )
    owned = (
        lax.psum_scatter(grad_gains, "fsdp", scatter_dimension=1, tiled=True),
        lax.psum_scatter(grad_shifts, "fsdp", scatter_dimension=1, tiled=True),
        lax.psum_scatter(grad_qkv, "fsdp", scatter_dimension=0, tiled=True),
        lax.psum_scatter(grad_out_proj, "fsdp", scatter_dimension=0, tiled=True),
        lax.psum_scatter(grad_up, "fsdp", scatter_dimension=0, tiled=True),
        lax.psum_scatter(grad_bias_up, "fsdp", scatter_dimension=0, tiled=True),
        lax.psum_scatter(grad_down, "fsdp", scatter_dimension=0, tiled=True),
    )
    summed = lax.psum((owned[0], owned[1], owned[2], owned[3], owned[4], owned[5], owned[6]), "dp")
    return (
        block_out,
        d_inputs,
        summed[0],
        summed[1],
        summed[2],
        summed[3],
        summed[4],
        summed[5],
        summed[6],
    )


def solution(mesh):
    placed = (
        P(("fsdp", "dp"), None),
        P(("fsdp", "dp")),
        P(None, "fsdp"),
        P(None, "fsdp"),
        P("fsdp", None),
        P("fsdp", None),
        P("fsdp", None),
        P("fsdp"),
        P("fsdp", None),
        P(("fsdp", "dp"), None),
    )
    return jax.shard_map(
        per_device,
        mesh=mesh,
        in_specs=placed,
        out_specs=(
            P(("fsdp", "dp"), None),
            P(("fsdp", "dp"), None),
            P(None, "fsdp"),
            P(None, "fsdp"),
            P("fsdp", None),
            P("fsdp", None),
            P("fsdp", None),
            P("fsdp"),
            P("fsdp", None),
        ),
        check_vma=False,
    )
```

profile of v0, /device:TPU:0, one launch (start us, length us, event | category | flops | bytes accessed | tf_op | source)
XLA Modules:
  0.0 1196.6 jit_solution(12556076253939985790)
XLA Ops:
  11.4 22.7 %all-gather = bf16[8,96,2]{1,2,0:T(2,128)(2,1)S(1)} all-gather(bf16[1,96,2]{1,2,0:T(2,128)(2,1)} %bitcast.158), channel_id=1, replica_groups=mesh['fsdp'=8,'dp'=4] {'fsdp'}, dimensions={0}, use_global_device_ids=true | all-gather | bytes 3456 | tf_op jit(solution)/shard_map/all_gather | solution.py:93
  34.9 26.7 %all-gather.2 = bf16[8,1,384]{2,1,0:T(2,128)(2,1)S(1)} all-gather(bf16[1,1,384]{2,1,0:T(2,128)(2,1)S(1)} %reshape.237), channel_id=1, replica_groups=mesh['fsdp'=8,'dp'=4] {'fsdp'}, dimensions={0}, use_global_device_ids=true | all-gather | bytes 6912 | tf_op jit(solution)/shard_map/all_gather | solution.py:98
  62.2 26.7 %all-gather.1 = bf16[8,96,6]{1,2,0:T(8,128)(2,1)S(1)} all-gather(bf16[1,96,6]{1,2,0:T(8,128)(2,1)} %bitcast.157), channel_id=1, replica_groups=mesh['fsdp'=8,'dp'=4] {'fsdp'}, dimensions={0}, use_global_device_ids=true | all-gather | bytes 10368 | tf_op jit(solution)/shard_map/all_gather | solution.py:94
  89.6 1.8 copy.79
  93.9 6.4 add_convert_fusion
  103.5 1.8 copy.83
  108.2 76.9 %while.27 = (s32[]{:T(128)}, bf16[2,512,768]{2,1,0:T(8,128)(2,1)}, f32[2,12,512]{2,1,0:T(8,128)S(1)}, s32[2,512]{1,0:T(2,128)S(1)}, s32[1024]{0:T(1024)S(1)}, /*...) while((s32[]{:T(128)}, bf16[2,512,768]{2,1,0:T(8,128)(2,1)}, ...), condition=%wide.region_5.6_spmd, body=%wide.region_2.5_spmd.sunk | while | flops 1686628352 | bytes 187926672 | solution.py:129
  109.7 10.6 fusion.103
  120.3 12.8 %fusion.104 = f32[12,512]{1,0:T(8,128)S(1)} fusion(f32[12,512,1024]{2,1,0:T(8,128)} %get-tuple-element.454, f32[12,512]{1,0:T(8,128)S(1)} %get-tuple-element.455, pred[512,1024]{1,0:T(8,128)(4,1)S(1)} %broadcast_compare_fusion.4), kind=kLoop, calls=%fused_computation.4.clone.1 | loop fusion | flops 25159680 | bytes 25739264 | tf_op jit(solution)/shard_map/while/body/eval_jaxpr/reduce_sum | solution.py:56
  133.1 3.2 copy-done
  136.3 9.0 fusion.105
  148.1 10.9 fusion.103
  159.1 12.4 %fusion.104 = f32[12,512]{1,0:T(8,128)S(1)} fusion(f32[12,512,1024]{2,1,0:T(8,128)} %get-tuple-element.454, f32[12,512]{1,0:T(8,128)S(1)} %get-tuple-element.455, pred[512,1024]{1,0:T(8,128)(4,1)S(1)} %broadcast_compare_fusion.4), kind=kLoop, calls=%fused_computation.4.clone.1 | loop fusion | flops 25159680 | bytes 25739264 | tf_op jit(solution)/shard_map/while/body/eval_jaxpr/reduce_sum | solution.py:56
  171.4 3.2 copy-done
  174.6 9.0 fusion.105
  185.1 4.0 fusion.49
  191.1 9.1 all-gather.12.cloned.1.call-done
  200.3 11.2 fusion.43
  211.4 68.6 %all-gather.14.cloned.1.call-done = bf16[3072,768]{1,0:T(8,128)(2,1)} async-done(((bf16[384,768]{1,0:T(8,128)(2,1)}), bf16[3072,768]{1,0:T(8,128)(2,1)}) %all-gather.14.cloned.1.call-update) | async-done | bytes 4718608 | tf_op jit(solution)/shard_map/all_gather | solution.py:99
  280.0 17.9 %convert_reduce_fusion = (f32[3072]{0:T(1024)}, bf16[1024,3072]{1,0:T(8,128)(2,1)S(1)}) fusion(f32[1024,3072]{1,0:T(8,128)} %fusion.43, f32[3072]{0:T(1024)S(1)} %bitcast.154, bf16[1024,768]{1,0:T(8,128)(2,1)S(1)} %copy-done.24, bf16[3072,768]{1,0:T(8,128)(2,1)} %all-gather.14.cloned.1.call-done), kind=kOutput, calls=%fused_computation.41 | convolution fusion | flops 4916769792 | bytes 25190400 | tf_op jit(solution)/shard_map/dot_general | solution.py:34
  298.0 7.3 fusion.51
  305.3 3.5 copy.88
  308.8 4.5 multiply_reduce_fusion.1
  316.8 2.8 fusion.53
  319.7 3.9 convolution_convert_fusion
  324.8 179.7 %while.28 = (s32[]{:T(128)}, f32[1024,768]{0,1:T(8,128)}, f32[1024,768]{0,1:T(8,128)}, bf16[2,512,768]{2,1,0:T(8,128)(2,1)}, bf16[2,512,768]{1,2,0:T(8,128)(2,1)...) while((s32[]{:T(128)}, f32[1024,768]{0,1:T(8,128)}, ...), condition=%wide.region_12.13_spmd.clone, body=%wide.region_10.12_spmd.clone.sunk | while | flops 4126140416 | bytes 298764608 | solution.py:175
  329.2 10.3 fusion.116
  339.4 13.3 %fusion.117 = f32[12,64,1024]{2,1,0:T(8,128)} fusion(bf16[512,12,64]{0,2,1:T(8,128)(2,1)S(1)} %bitcast.137, f32[12,512,1024]{2,1,0:T(8,128)} %fusion.116, f32[12,512]{1,0:T(8,128)S(1)} %dynamic-slice_bitcast_fusion.2, pred[512,1024]{1,0:T(8,128)(4,1)S(1)} %broadcast_compare_fusion.5), kind=kOutput, calls=%fused_computation.17.clone.1 | convolution fusion | flops 830472192 | bytes 29646848 | tf_op jit(solution)/shard_map/while/body/eval_jaxpr/hqk,qhd->khd/dot_general | solution.py:69
  352.7 18.1 %multiply_reduce_fusion.5 = (f32[12,512]{1,0:T(8,128)S(1)}, f32[12,512,1024]{2,1,0:T(8,128)}) fusion(f32[12,512,1024]{2,1,0:T(8,128)} %fusion.116, f32[12,512]{1,0:T(8,128)S(1)} %dynamic-slice_bitcast_fusion.2, pred[512,1024]{1,0:T(8,128)(4,1)S(1)} %broadcast_compare_fusion.5, bf16[512,12,64]{0,2,1:T(8,128)(2,1)} %bitcast.136, ...), kind=kOutput, calls=%fused_computation.14.clone.1 | convolution fusion | flops 836757504 | bytes 53264384 | tf_op jit(solution)/shard_map/while/body/eval_jaxpr/qhd,khd->hqk/dot_general | solution.py:70
  370.8 21.8 %multiply_convert_fusion.2 = bf16[12,512,1024]{2,1,0:T(8,128)(2,1)} fusion(f32[12,512,1024]{2,1,0:T(8,128)} %get-tuple-element.467, f32[12,512,1024]{2,1,0:T(8,128)} %fusion.116, f32[12,512]{1,0:T(8,128)S(1)} %get-tuple-element.468, f32[12,512]{1,0:T(8,128)S(1)} %dynamic-slice_bitcast_fusion.2, pred[512,1024]{1,0:T(8,128)(4,1)S(1)} %broadcast_compare_fusion.5), kind=kLoop, calls=%fused_computation.13.clone.1 | loop fusion | flops 37748736 | bytes 63488000 | tf_op jit(solution)/shard_map/while/body/eval_jaxpr/convert_element_type | solution.py:74
  392.6 8.5 convolution_multiply_fusion.5
  401.1 7.0 convolution_multiply_fusion.4
  408.4 2.3 bitcast_add_fusion.3
  410.7 1.7 copy-done.2
  419.2 10.1 fusion.116
  429.3 13.0 %fusion.117 = f32[12,64,1024]{2,1,0:T(8,128)} fusion(bf16[512,12,64]{0,2,1:T(8,128)(2,1)S(1)} %bitcast.137, f32[12,512,1024]{2,1,0:T(8,128)} %fusion.116, f32[12,512]{1,0:T(8,128)S(1)} %dynamic-slice_bitcast_fusion.2, pred[512,1024]{1,0:T(8,128)(4,1)S(1)} %broadcast_compare_fusion.5), kind=kOutput, calls=%fused_computation.17.clone.1 | convolution fusion | flops 830472192 | bytes 29646848 | tf_op jit(solution)/shard_map/while/body/eval_jaxpr/hqk,qhd->khd/dot_general | solution.py:69
  442.3 18.1 %multiply_reduce_fusion.5 = (f32[12,512]{1,0:T(8,128)S(1)}, f32[12,512,1024]{2,1,0:T(8,128)}) fusion(f32[12,512,1024]{2,1,0:T(8,128)} %fusion.116, f32[12,512]{1,0:T(8,128)S(1)} %dynamic-slice_bitcast_fusion.2, pred[512,1024]{1,0:T(8,128)(4,1)S(1)} %broadcast_compare_fusion.5, bf16[512,12,64]{0,2,1:T(8,128)(2,1)} %bitcast.136, ...), kind=kOutput, calls=%fused_computation.14.clone.1 | convolution fusion | flops 836757504 | bytes 53264384 | tf_op jit(solution)/shard_map/while/body/eval_jaxpr/qhd,khd->hqk/dot_general | solution.py:70
  460.4 21.2 %multiply_convert_fusion.2 = bf16[12,512,1024]{2,1,0:T(8,128)(2,1)} fusion(f32[12,512,1024]{2,1,0:T(8,128)} %get-tuple-element.467, f32[12,512,1024]{2,1,0:T(8,128)} %fusion.116, f32[12,512]{1,0:T(8,128)S(1)} %get-tuple-element.468, f32[12,512]{1,0:T(8,128)S(1)} %dynamic-slice_bitcast_fusion.2, pred[512,1024]{1,0:T(8,128)(4,1)S(1)} %broadcast_compare_fusion.5), kind=kLoop, calls=%fused_computation.13.clone.1 | loop fusion | flops 37748736 | bytes 63488000 | tf_op jit(solution)/shard_map/while/body/eval_jaxpr/convert_element_type | solution.py:74
  481.7 8.5 convolution_multiply_fusion.5
  490.2 7.0 convolution_multiply_fusion.4
  497.5 2.3 bitcast_add_fusion.3
  499.8 1.7 copy-done.2
  504.6 3.2 copy.94
  509.5 9.8 fusion.31
  520.7 12.9 %fusion.44 = f32[3072,768]{1,0:T(8,128)} fusion(bf16[1024,768]{1,0:T(8,128)(2,1)S(1)} %copy-done.25, f32[1024,3072]{1,0:T(8,128)} %fusion.43, f32[3072]{0:T(1024)S(1)} %bitcast.155), kind=kOutput, calls=%fused_computation.105 | convolution fusion | flops 4863295488 | bytes 23605248 | tf_op jit(solution)/shard_map/dot_general | solution.py:28
  533.7 1.8 copy-done.12
  535.5 10.5 fusion.42
  548.0 8.0 fusion.50
  556.0 4.0 copy.96
  560.0 2.6 fusion.29
  566.9 6.4 convert_reduce_fusion.2
  573.4 1.8 convert_reduce_fusion.3
  577.6 69.8 %reduce-scatter.11.cloned.1.call-done = f32[96,2304]{1,0:T(8,128)} async-done(((f32[768,2304]{1,0:T(8,128)}), f32[96,2304]{1,0:T(8,128)}) %reduce-scatter.11.cloned.1.call-update) | async-done | bytes 884752 | tf_op jit(solution)/shard_map/reduce_scatter | solution.py:200
  647.5 164.9 %reduce-scatter.17.cloned.1.call-done = f32[384,768]{1,0:T(8,128)} async-done(((f32[3072,768]{1,0:T(8,128)}), f32[384,768]{1,0:T(8,128)}) %reduce-scatter.17.cloned.1.call-update) | async-done | bytes 1179664 | tf_op jit(solution)/shard_map/reduce_scatter | solution.py:204
  812.4 164.8 %reduce-scatter.15.cloned.1.call-done = f32[96,3072]{1,0:T(8,128)} async-done(((f32[768,3072]{1,0:T(8,128)}), f32[96,3072]{1,0:T(8,128)}) %reduce-scatter.15.cloned.1.call-update) | async-done | bytes 1179664 | tf_op jit(solution)/shard_map/reduce_scatter | solution.py:202
  977.2 11.5 add_convert_fusion.1
  988.7 2.7 copy.99
  991.5 2.4 copy.100
  993.8 35.2 %all-reduce = f32[3072]{0:T(1024)S(1)} all-reduce(f32[3072]{0:T(1024)S(1)} %copy-done.51), channel_id=7, replica_groups=mesh['fsdp'=8,'dp'=4] {'fsdp'}, use_global_device_ids=true, to_apply=%region_34.35.clone | all-reduce | flops 3072 | bytes 24576
  1029.1 13.2 %reduce-scatter.19.cloned.1.call-done = f32[96,2]{1,0:T(8,128)} async-done(((f32[768,2]{1,0:T(8,128)}), f32[96,2]{1,0:T(8,128)}) %reduce-scatter.19.cloned.1.call-update) | async-done | bytes 784
  1043.2 64.1 %reduce-scatter.21.cloned.1.call-done = f32[96,6]{1,0:T(8,128)} async-done(((f32[768,6]{1,0:T(8,128)}), f32[96,6]{1,0:T(8,128)}) %reduce-scatter.21.cloned.1.call-update) | async-done | bytes 2320
  1108.1 6.3 all-reduce.1
  1114.4 69.4 %all-reduce.5.cloned.1.call-done = (f32[96,2304]{1,0:T(8,128)}, f32[96,768]{1,0:T(8,128)}, f32[96,3072]{1,0:T(8,128)}, f32[384,768]{1,0:T(8,128)}) async-done(((f32[96,2304]{1,0:T(8,128)}, f32[96,768]{1,0:T(8,128)}, f32[96,3072]{1,0:T(8,128)}, f32[384,768]{1,0:T(8,128)}), (f32[96,2304]{1,0:T(8,128)}, f32[96,768]{1,0:T(8,128)}, f32[96,3072]{1,0:T(8,128)}, f32[384,768]{1,0:T(8,128)})) %all-reduce.5.cloned.1.call-update) | async-done | bytes 3538960 | tf_op jit(solution)/shard_map/psum | solution.py:206
  1183.8 2.3 copy.164
  (235 shorter events, 57.7 us)
Async XLA Ops:
  7.2 86.7 %all-gather.8.cloned.1.call-start = ((), (), s32[]{:S(2)}) async-start(), calls=%async_computation.6 | async-start | bytes 3981312 | tf_op jit(solution)/shard_map/all_gather | solution.py:95
  7.9 177.1 %all-gather.10.cloned.1.call-start = ((), (), s32[]{:S(2)}) async-start(), calls=%async_computation.7 | async-start | bytes 1327104 | tf_op jit(solution)/shard_map/all_gather | solution.py:96
  8.7 191.6 %all-gather.12.cloned.1.call-start = ((), (), s32[]{:S(2)}) async-start(), calls=%async_computation.8 | async-start | bytes 5308416 | tf_op jit(solution)/shard_map/all_gather | solution.py:97
  9.4 270.6 %all-gather.14.cloned.1.call-start = ((), (), s32[]{:S(2)}) async-start(), calls=%async_computation.9 | async-start | bytes 5308416 | tf_op jit(solution)/shard_map/all_gather | solution.py:99
  10.0 567.7 %reduce-scatter.13.cloned.1.call-start = ((), (), s32[]{:S(2)}) async-start(), calls=%async_computation.11 | async-start | bytes 2654208 | tf_op jit(solution)/shard_map/reduce_scatter | solution.py:201
  34.9 59.1 %copy-start.40 = (f32[768]{0:T(1024)}, f32[768]{0:T(1024)S(1)}, u32[]{:S(2)}) copy-start(f32[768]{0:T(1024)S(1)} %get-tuple-element.277) | copy-start | bytes 9220
  89.6 4.3 copy-start.54
  89.6 2.6 copy-start.23
  91.5 2.5 copy-start.8
  91.8 8.6 copy-start.38
  92.2 8.2 copy-start.44
  92.2 8.1 copy-start.42
  105.3 2.9 copy-start.31
  108.1 76.9 %copy-start.56 = (f32[768]{0:T(1024)S(1)}, f32[768]{0:T(1024)}, u32[]{:S(2)}) copy-start(f32[768]{0:T(1024)} %get-tuple-element.272) | copy-start | bytes 9220
  120.3 16.0 %copy-start = (f32[12,512,1024]{2,1,0:T(8,128)S(1)}, f32[12,512,1024]{2,1,0:T(8,128)}, u32[]{:S(2)}) copy-start(f32[12,512,1024]{2,1,0:T(8,128)} %get-tuple-element.454) | copy-start | bytes 75497472 | tf_op jit(solution)/shard_map/while
  159.1 15.5 %copy-start = (f32[12,512,1024]{2,1,0:T(8,128)S(1)}, f32[12,512,1024]{2,1,0:T(8,128)}, u32[]{:S(2)}) copy-start(f32[12,512,1024]{2,1,0:T(8,128)} %get-tuple-element.454) | copy-start | bytes 75497472 | tf_op jit(solution)/shard_map/while
  189.1 11.2 copy-start.32
  189.1 11.2 copy-start.36
  189.1 124.2 %copy-start.29 = (f32[1024]{0:T(1024)}, f32[1024]{0:T(1024)S(1)}, u32[]{:S(2)}) copy-start(f32[1024]{0:T(1024)S(1)} %broadcast_multiply_fusion) | copy-start | bytes 12292
  191.1 122.2 %copy-start.34 = (f32[1024]{0:T(1024)}, f32[1024]{0:T(1024)S(1)}, u32[]{:S(2)}) copy-start(f32[1024]{0:T(1024)S(1)} %fusion.37) | copy-start | bytes 12292
  200.2 79.8 %copy-start.24 = (bf16[1024,768]{1,0:T(8,128)(2,1)S(1)}, bf16[1024,768]{1,0:T(8,128)(2,1)}, u32[]{:S(2)}) copy-start(bf16[1024,768]{1,0:T(8,128)(2,1)} %param.23) | copy-start | bytes 4718596
  200.2 79.8 %copy-start.49 = (f32[8,1,384]{2,1,0:T(1,128)S(1)}, f32[8,1,384]{2,1,0:T(1,128)}, u32[]{:S(2)}) copy-start(f32[8,1,384]{2,1,0:T(1,128)} %convert_element_type.84) | copy-start | bytes 36868
  280.0 17.9 %copy-start.22 = (bf16[768,3072]{1,0:T(8,128)(2,1)S(1)}, bf16[768,3072]{1,0:T(8,128)(2,1)}, u32[]{:S(2)}) copy-start(bf16[768,3072]{1,0:T(8,128)(2,1)} %all-gather.12.cloned.1.call-done) | copy-start | bytes 14155780
  298.0 7.3 copy-start.58
  308.8 4.5 copy-start.11
  308.8 4.7 copy-start.16
  314.9 1.9 copy-start.26
  319.7 327.8 %reduce-scatter.11.cloned.1.call-start = ((), (), s32[]{:S(2)}) async-start(), calls=%async_computation.10 | async-start | bytes 7962624 | tf_op jit(solution)/shard_map/reduce_scatter | solution.py:200
  329.2 10.3 copy-start.7
  401.1 7.1 copy-start.1
  401.1 7.1 copy-start.4
  401.1 7.3 copy-start.6
  410.7 1.8 copy-start.2
  419.2 10.1 copy-start.7
  490.2 7.1 copy-start.1
  490.2 7.1 copy-start.4
  490.2 7.3 copy-start.6
  499.8 1.8 copy-start.2
  504.5 3.3 copy-start.3
  507.8 1.7 copy-start.55
  519.4 293.0 %reduce-scatter.17.cloned.1.call-start = ((), (), s32[]{:S(2)}) async-start(), calls=%async_computation.13 | async-start | bytes 10616832 | tf_op jit(solution)/shard_map/reduce_scatter | solution.py:204
  533.6 1.9 copy-start.12
  533.6 1.9 copy-start.30
  533.6 1.9 copy-start.33
  533.6 1.9 copy-start.35
  533.6 1.9 copy-start.37
  533.6 443.5 %reduce-scatter.15.cloned.1.call-start = ((), (), s32[]{:S(2)}) async-start(), calls=%async_computation.12 | async-start | bytes 10616832 | tf_op jit(solution)/shard_map/reduce_scatter | solution.py:202
  546.0 1.9 copy-start.21
  546.0 496.3 %reduce-scatter.19.cloned.1.call-start = ((), (), s32[]{:S(2)}) async-start(), calls=%async_computation.14 | async-start | bytes 442368
  556.0 4.0 copy-start.9
  560.0 2.6 copy-start.45
  560.0 2.9 copy-start.14
  562.8 4.0 copy-start.18
  562.8 4.0 copy-start.47
  566.9 8.4 copy-start.52
  566.9 9.5 copy-start.57
  573.3 403.9 %copy-start.13 = (f32[1024,768]{0,1:T(8,128)S(1)}, f32[1024,768]{0,1:T(8,128)}, u32[]{:S(2)}) copy-start(f32[1024,768]{0,1:T(8,128)} %copy-done.10) | copy-start | bytes 9437188
  573.3 403.9 %copy-start.53 = (f32[768]{0:T(1024)S(1)}, f32[768]{0:T(1024)}, u32[]{:S(2)}) copy-start(f32[768]{0:T(1024)} %get-tuple-element.271) | copy-start | bytes 9220
  573.3 533.9 %reduce-scatter.21.cloned.1.call-start = ((), (), s32[]{:S(2)}) async-start(), calls=%async_computation.15 | async-start | bytes 442368
  576.3 607.5 %all-reduce.5.cloned.1.call-start = ((), (), s32[]{:S(2)}) async-start(), calls=%async_computation.16 | async-start | bytes 7077888 | tf_op jit(solution)/shard_map/psum | solution.py:206
  988.7 2.7 copy-start.19
  991.5 2.4 copy-start.51
  1183.8 4.0 copy-start.28
  1183.8 5.0 copy-start.27
  (13 other events, 19.7 us)
Sparse Core Ops, SparseCore 0:
  10.2 67.5 all-gather.7
  79.9 40.0 all-gather.9
  122.2 78.0 all-gather.11
  202.3 77.6 all-gather.13
  319.8 68.1 reduce-scatter.12
  519.5 127.9 reduce-scatter.10
  651.1 161.2 reduce-scatter.16
  816.0 161.1 reduce-scatter.14
  981.0 61.2 reduce-scatter.18
  1046.0 61.2 reduce-scatter.20
  1109.9 73.9 all-reduce.4
where the time goes:
time: 1210 us; the launch traced here: 1200 us
  waiting for transfers between devices  627 us (52%)
  matrix products  260 us (21%)
  blocking collectives  118 us (10%)
  other arithmetic  95.8 us (8%)
  local copies, waits for them, and re-layouts  80.1 us (7%)
  between operations  15.3 us (1%)
    reduce_scatter x1, waiting for transfers between devices, per_device(): lax.psum_scatter(grad_down, 'fsdp', scatter_dimension=0, tiled=True)  165 us
    reduce_scatter x1, waiting for transfers between devices, per_device(): lax.psum_scatter(grad_up, 'fsdp', scatter_dimension=0, tiled=True)  165 us
    unnamed x13, waiting for transfers between devices  80 us
    reduce_scatter x1, waiting for transfers between devices, per_device(): lax.psum_scatter(grad_qkv, 'fsdp', scatter_dimension=0, tiled=True)  69.8 us
    psum x1, waiting for transfers between devices, per_device(): lax.psum((owned[0], owned[1], owned[2], owned[3], owned[4], owned[5], own...  69.4 us
    all_gather x1, waiting for transfers between devices, per_device(): lax.all_gather(w_down, 'fsdp', axis=0, tiled=True)  68.6 us
    convert_element_type x2, other arithmetic, attend_backward(): d_scores = (attn_probs * (d_probs - inner)).astype(jnp.bfloat16)  43 us
    dot_general x4, matrix products, block_scores(): jnp.einsum('qhd,khd->hqk', split_heads(query), split_heads(keys), preferr...  41.8 us
  transfers between devices with their start and end apart: 11, of which 8 were waited for; matrix products, arithmetic and copies ran while one was open for 31% of the time, Pallas kernels for 0%

commit v1 on v0

--- a/solution.py
+++ b/solution.py
@@ -1,9 +1,403 @@
+import functools
 import math
 
 import jax
 import jax.numpy as jnp
 from jax import lax
+from jax.experimental import pallas as pl
+from jax.experimental.pallas import tpu as pltpu
 from jax.sharding import PartitionSpec as P
+
+MESH = pl.DeviceIdType.MESH
+F32 = jnp.float32
+BF16 = jnp.bfloat16
+
+
+class Place:
+    def __init__(self):
+        f = lax.axis_index("fsdp")
+        d = lax.axis_index("dp")
+        self.f, self.d = f, d
+        self.z, self.x = f // 2, f % 2
+        self.y, self.c = d // 2, d % 2
+
+    def at(self, z=None, x=None, y=None, c=None):
+        z = self.z if z is None else z
+        x = self.x if x is None else x
+        y = self.y if y is None else y
+        c = self.c if c is None else c
+        return (z * 2 + x, y * 2 + c)
+
+    def z_to(self, k):
+        return (self.z + k) % 4
+
+    def z_from(self, k):
+        return (self.z + 4 - k) % 4
+
+
+def copy_to(src, dst, send, recv, device):
+    return pltpu.make_async_remote_copy(
+        src_ref=src, dst_ref=dst, send_sem=send, recv_sem=recv, device_id=device, device_id_type=MESH
+    )
+
+
+def greet(place):
+    barrier = pltpu.get_barrier_semaphore()
+    others = [place.at(z=place.z_to(k)) for k in (1, 2, 3)]
+    others += [place.at(z=place.z_to(k), x=1 - place.x) for k in (0, 1, 2, 3)]
+    others += [place.at(y=1 - place.y), place.at(c=1 - place.c)]
+    for other in others:
+        pl.semaphore_signal(barrier, inc=1, device_id=other, device_id_type=MESH)
+    pl.semaphore_wait(barrier, len(others))
+
+
+class Gather:
+    def __init__(self, place, chunks, send, recv):
+        self.p, self.chunks, self.send, self.recv = place, chunks, send, recv
+        self.sent = []
+
+    def view(self, k, f, start, width):
+        src, full, rows, row, col = self.chunks[k]
+        return full.at[pl.ds(pl.multiple_of(f * rows + row, 32), 96), pl.ds(pl.multiple_of(col + start, 128), width)]
+
+    def own(self, k, start, width):
+        src, full, rows, row, col = self.chunks[k]
+        return src.at[pl.ds(row, 96), pl.ds(pl.multiple_of(col + start, 128), width)]
+
+    def put(self, k, slot, src, dst, device):
+        copy = copy_to(src, dst, self.send.at[k, slot], self.recv.at[k, slot], device)
+        copy.start()
+        self.sent.append(copy)
+
+    def got(self, k, slot, dst):
+        copy_to(dst, dst, self.send.at[k, slot], self.recv.at[k, slot], self.p.at(c=1 - self.p.c)).wait_recv()
+
+    def ab(self):
+        return self.p.c * 384 + self.p.y * 128
+
+    def mine(self):
+        return self.p.c * 384 + self.p.y * 256
+
+    def theirs(self):
+        return self.p.c * 384 + (1 - self.p.y) * 256
+
+    def half(self):
+        return self.p.c * 384
+
+    def start(self, k):
+        p = self.p
+        src = self.own(k, self.ab(), 256)
+        dst = self.view(k, p.f, self.ab(), 256)
+        for hop in (1, 2, 3):
+            self.put(k, hop - 1, src, dst, p.at(z=p.z_to(hop)))
+        self.put(k, 3, src, dst, p.at(x=1 - p.x))
+
+    def z_event(self, k, hop):
+        p = self.p
+        f = p.z_from(hop) * 2 + p.x
+        ab = self.view(k, f, self.ab(), 256)
+        self.got(k, hop - 1, ab)
+        self.put(k, 3 + hop, ab, ab, p.at(x=1 - p.x))
+        b = self.view(k, f, self.mine(), 128)
+        self.put(k, 7 + hop - 1, b, b, p.at(y=1 - p.y))
+
+    def x_event(self, k, hop):
+        p = self.p
+        f = p.z_from(hop) * 2 + 1 - p.x
+        self.got(k, 3 + hop, self.view(k, f, self.ab(), 256))
+        b = self.view(k, f, self.mine(), 128)
+        self.put(k, 10 + hop, b, b, p.at(y=1 - p.y))
+
+    def source(self, j):
+        p = self.p
+        return p.z_from(j + 1) * 2 + p.x if j < 3 else p.z_from(j - 3) * 2 + 1 - p.x
+
+    def y_event(self, k, j):
+        p = self.p
+        f = self.source(j)
+        self.got(k, 7 + j, self.view(k, f, self.theirs(), 128))
+        h = self.view(k, f, self.half(), 384)
+        self.put(k, 14 + j, h, h, p.at(c=1 - p.c))
+
+    def c_event(self, k, j):
+        p = self.p
+        self.got(k, 14 + j, self.view(k, self.source(j), (1 - p.c) * 384, 384))
+
+    def finish(self):
+        for copy in self.sent:
+            copy.wait_send()
+
+
+class Reduce:
+    def __init__(self, place, k, grads, bufs, final, send, recv):
+        self.p, self.k, self.g, self.b, self.out = place, k, grads, bufs, final
+        self.send, self.recv = send, recv
+        self.sent = []
+        self.slot_a = 3 * place.c + 1
+        self.slot_b = 3 * place.c + 2 * place.y
+        self.slot_o = 3 * place.c + 2 * (1 - place.y)
+
+    def put(self, s, src, dst, device):
+        copy = copy_to(src, dst, self.send.at[self.k, s], self.recv.at[self.k, s], device)
+        copy.start()
+        self.sent.append(copy)
+
+    def got(self, s, dst):
+        copy_to(dst, dst, self.send.at[self.k, s], self.recv.at[self.k, s], self.p.at(c=1 - self.p.c)).wait_recv()
+
+    def add(self, dst, src):
+        dst[...] = (dst[...].astype(F32) + src[...].astype(F32)).astype(BF16)
+
+    def e0(self):
+        p = self.p
+        self.put(0, self.g.at[pl.ds(3 * (1 - p.c), 3)], self.b["c"], p.at(c=1 - p.c))
+
+    def e1(self):
+        p = self.p
+        self.got(0, self.b["c"])
+        base = 3 * p.c
+
+        def body(i, _):
+            s, z = i // 4, i % 4
+            for x in (0, 1):
+                self.add(self.g.at[base + s, z, x], self.b["c"].at[s, z, x])
+            return 0
+
+        lax.fori_loop(0, 12, body, 0)
+        self.put(1, self.g.at[3 * p.c + 2 * (1 - p.y)], self.b["y"], p.at(y=1 - p.y))
+        self.put(2, self.g.at[self.slot_a, :, 1 - p.x], self.b["xa"], p.at(x=1 - p.x))
+
+    def x_add(self, slot, s, buf):
+        p = self.p
+        self.got(s, buf)
+
+        def body(z, _):
+            self.add(self.g.at[slot, z, p.x], buf.at[z])
+            return 0
+
+        lax.fori_loop(0, 4, body, 0)
+
+    def z_put(self, slot, s, buf):
+        p = self.p
+        for hop in (1, 2, 3):
+            z = p.z_to(hop)
+            self.put(s + hop - 1, self.g.at[slot, z, p.x], buf.at[hop - 1], p.at(z=z))
+
+    def z_sum(self, slot, s, buf):
+        p = self.p
+        total = self.g[slot, p.z, p.x].astype(F32)
+        for hop in (1, 2, 3):
+            self.got(s + hop - 1, buf.at[hop - 1])
+            total = total + buf[hop - 1].astype(F32)
+        return total.astype(BF16)
+
+    def e2(self):
+        self.x_add(self.slot_a, 2, self.b["xa"])
+        self.z_put(self.slot_a, 3, self.b["za"])
+
+    def e3(self):
+        p = self.p
+        self.got(1, self.b["y"])
+
+        def body(z, _):
+            for x in (0, 1):
+                self.add(self.g.at[self.slot_b, z, x], self.b["y"].at[z, x])
+            return 0
+
+        lax.fori_loop(0, 4, body, 0)
+        self.put(6, self.g.at[self.slot_b, :, 1 - p.x], self.b["xb"], p.at(x=1 - p.x))
+
+    def e4(self):
+        p = self.p
+        self.b["pa"][...] = self.z_sum(self.slot_a, 3, self.b["za"])
+        self.put(7, self.b["pa"], self.b["ya"], p.at(y=1 - p.y))
+
+    def e5(self):
+        self.x_add(self.slot_b, 6, self.b["xb"])
+        self.z_put(self.slot_b, 8, self.b["zb"])
+
+    def e6(self):
+        p = self.p
+        self.out[self.slot_b] = self.z_sum(self.slot_b, 8, self.b["zb"])
+        self.put(11, self.out.at[self.slot_b], self.out.at[self.slot_b], p.at(y=1 - p.y))
+
+    def e7(self):
+        self.got(7, self.b["ya"])
+        self.out[self.slot_a] = (self.b["pa"][...].astype(F32) + self.b["ya"][...].astype(F32)).astype(BF16)
+
+    def e8(self):
+        p = self.p
+        self.got(11, self.out.at[self.slot_o])
+        half = self.out.at[pl.ds(3 * p.c, 3)]
+        self.put(12, half, half, p.at(c=1 - p.c))
+
+    def e9(self):
+        self.got(12, self.out.at[pl.ds(3 * (1 - self.p.c), 3)])
+
+    def finish(self):
+        for copy in self.sent:
+            copy.wait_send()
+
+    def events(self):
+        return [self.e0, self.e1, self.e2, self.e3, self.e4, self.e5, self.e6, self.e7, self.e8, self.e9]
+
+
+def reduce_bufs(r, w):
+    v = lambda *lead: pltpu.VMEM((*lead, r, w), BF16)
+    return dict(c=v(3, 4, 2), y=v(4, 2), xa=v(4), xb=v(4), za=v(3), zb=v(3), pa=v(), ya=v())
+
+
+BUF_NAMES = ("c", "y", "xa", "xb", "za", "zb", "pa", "ya")
+
+
+def gather_kernel(q_ref, o_ref, u_ref, d_ref, fq, fo, fu, fd, send, recv, local):
+    p = Place()
+    chunks = [(q_ref, fq, 96, 0, 768 * j) for j in range(3)]
+    chunks += [(o_ref, fo, 96, 0, 0)]
+    chunks += [(u_ref, fu, 96, 0, 768 * j) for j in range(4)]
+    chunks += [(d_ref, fd, 384, 96 * j, 0) for j in range(4)]
+    g = Gather(p, chunks, send, recv)
+    greet(p)
+    owns = []
+    for i, (src, dst, rows) in enumerate(((q_ref, fq, 96), (o_ref, fo, 96), (u_ref, fu, 96), (d_ref, fd, 384))):
+        copy = pltpu.make_async_copy(src, dst.at[pl.ds(pl.multiple_of(p.f * rows, 32), rows)], local.at[i])
+        copy.start()
+        owns.append(copy)
+    n = len(chunks)
+    stages = 5
+    for t in range(n + stages - 1):
+        for stage in range(stages):
+            k = t - stage
+            if not 0 <= k < n:
+                continue
+            if stage == 0:
+                g.start(k)
+            elif stage == 1:
+                for hop in (1, 2, 3):
+                    g.z_event(k, hop)
+            elif stage == 2:
+                for hop in (0, 1, 2, 3):
+                    g.x_event(k, hop)
+            elif stage == 3:
+                for j in range(7):
+                    g.y_event(k, j)
+            else:
+                for j in range(7):
+                    g.c_event(k, j)
+    for copy in owns:
+        copy.wait()
+    g.finish()
+
+
+def gather_weights(w_qkv, w_out, w_up, w_down):
+    args = (w_qkv, w_out, w_up, w_down)
+    hbm = pl.BlockSpec(memory_space=pl.ANY)
+    vmem = pl.BlockSpec(memory_space=pltpu.VMEM)
+    return pl.pallas_call(
+        gather_kernel,
+        out_shape=[jax.ShapeDtypeStruct((a.shape[0] * 8, a.shape[1]), BF16) for a in args],
+        in_specs=[hbm] * 4,
+        out_specs=[vmem] * 4,
+        scratch_shapes=[
+            pltpu.SemaphoreType.DMA((12, 21)),
+            pltpu.SemaphoreType.DMA((12, 21)),
+            pltpu.SemaphoreType.DMA((4,)),
+        ],
+        compiler_params=pltpu.CompilerParams(
+            collective_id=0, has_side_effects=True, vmem_limit_bytes=60 << 20
+        ),
+        name="gather",
+    )(*args)
+
+
+def reduce_kernel(d_ref, u_ref, o_ref, q_ref, od, ou, oo, oq, gd, gu, go, gq, fd, fx, *rest):
+    nb = len(BUF_NAMES)
+    bd = [dict(zip(BUF_NAMES, rest[:nb]))]
+    bx = dict(zip(BUF_NAMES, rest[nb : 2 * nb]))
+    send, recv, local = rest[2 * nb :]
+    p = Place()
+    sel = lambda bufs, j: {n: r.at[j] for n, r in bufs.items()}
+    chunks = []
+    loads = []
+    for j in range(3):
+        chunks.append(Reduce(p, j, gd.at[j], sel(bd[0], j), fd.at[j], send, recv))
+        for s in range(6):
+            loads.append((d_ref.at[:, :, s, :, pl.ds(256 * j, 256)], gd.at[j, s]))
+    for j in range(4):
+        chunks.append(Reduce(p, 3 + j, gu.at[j], sel(bx, j), fx.at[j], send, recv))
+        for s in range(6):
+            loads.append((u_ref.at[:, :, :, pl.ds(768 * j + 128 * s, 128)], gu.at[j, s]))
+    chunks.append(Reduce(p, 7, go.at[0], sel(bx, 4), fx.at[4], send, recv))
+    for s in range(6):
+        loads.append((o_ref.at[:, :, :, pl.ds(128 * s, 128)], go.at[0, s]))
+    for j in range(3):
+        chunks.append(Reduce(p, 8 + j, gq.at[j], sel(bx, 5 + j), fx.at[5 + j], send, recv))
+        for s in range(6):
+            col = (s // 2) * 768 + 256 * j + 128 * (s % 2)
+            loads.append((q_ref.at[:, :, :, pl.ds(col, 128)], gq.at[j, s]))
+    copies = [pltpu.make_async_copy(a, b, local.at[i]) for i, (a, b) in enumerate(loads)]
+    for copy in copies:
+        copy.start()
+    greet(p)
+    for copy in copies:
+        copy.wait()
+    n = len(chunks)
+    for t in range(n + 9):
+        for stage in range(9, -1, -1):
+            k = t - stage
+            if 0 <= k < n:
+                chunks[k].events()[stage]()
+    for chunk in chunks:
+        chunk.finish()
+    for j in range(3):
+        for s in range(6):
+            od[64 * s : 64 * s + 64, 256 * j : 256 * j + 256] = fd[j, s]
+    for j in range(4):
+        for s in range(6):
+            ou[:, 768 * j + 128 * s : 768 * j + 128 * s + 128] = fx[j, s]
+    for s in range(6):
+        oo[:, 128 * s : 128 * s + 128] = fx[4, s]
+    for j in range(3):
+        for s in range(6):
+            col = (s // 2) * 768 + 256 * j + 128 * (s % 2)
+            oq[:, col : col + 128] = fx[5 + j, s]
+
+
+def reduce_grads(gd, gu, go, gq):
+    hbm = pl.BlockSpec(memory_space=pl.ANY)
+    vmem = pl.BlockSpec(memory_space=pltpu.VMEM)
+    gd = gd.reshape(4, 2, 6, 64, 768)
+    gu = gu.reshape(4, 2, 96, 3072)
+    go = go.reshape(4, 2, 96, 768)
+    gq = gq.reshape(4, 2, 96, 2304)
+    lead = lambda n, r, w: [
+        pltpu.VMEM((n, *b.shape), BF16) for b in (reduce_bufs(r, w)[name] for name in BUF_NAMES)
+    ]
+    shapes = [(384, 768), (96, 3072), (96, 768), (96, 2304)]
+    return pl.pallas_call(
+        reduce_kernel,
+        out_shape=[jax.ShapeDtypeStruct(s, BF16) for s in shapes],
+        in_specs=[hbm] * 4,
+        out_specs=[vmem] * 4,
+        scratch_shapes=[
+            pltpu.VMEM((3, 6, 4, 2, 64, 256), BF16),
+            pltpu.VMEM((4, 6, 4, 2, 96, 128), BF16),
+            pltpu.VMEM((1, 6, 4, 2, 96, 128), BF16),
+            pltpu.VMEM((3, 6, 4, 2, 96, 128), BF16),
+            pltpu.VMEM((3, 6, 64, 256), BF16),
+            pltpu.VMEM((8, 6, 96, 128), BF16),
+            *lead(3, 64, 256),
+            *lead(8, 96, 128),
+            pltpu.SemaphoreType.DMA((11, 13)),
+            pltpu.SemaphoreType.DMA((11, 13)),
+            pltpu.SemaphoreType.DMA((66,)),
+        ],
+        compiler_params=pltpu.CompilerParams(
+            collective_id=1, has_side_effects=True, vmem_limit_bytes=60 << 20
+        ),
+        name="reduce",
+    )(gd, gu, go, gq)
+
 
 HEADS = 12
 HEAD = 64
@@ -88,15 +482,20 @@
     )
 
 
-def per_device(inputs, row_ids, ln_gains, biases, w_qkv, w_out, w_up, bias_up, w_down, cotangent):
+def per_device(fast, inputs, row_ids, ln_gains, biases, w_qkv, w_out, w_up, bias_up, w_down, cotangent):
+    weights = (w_qkv, w_out, w_up, w_down)
+    if fast:
+        whole = gather_weights(*weights)
+    else:
+        whole = [lax.all_gather(a, "fsdp", axis=0, tiled=True) for a in weights]
     gathered = (
         lax.all_gather(ln_gains, "fsdp", axis=1, tiled=True),
         lax.all_gather(biases, "fsdp", axis=1, tiled=True),
-        lax.all_gather(w_qkv, "fsdp", axis=0, tiled=True),
-        lax.all_gather(w_out, "fsdp", axis=0, tiled=True),
-        lax.all_gather(w_up, "fsdp", axis=0, tiled=True),
+        whole[0],
+        whole[1],
+        whole[2],
         lax.all_gather(bias_up, "fsdp", axis=0, tiled=True),
-        lax.all_gather(w_down, "fsdp", axis=0, tiled=True),
+        whole[3],
     )
     gains = gathered[0].astype(jnp.float32)
     shifts = gathered[1].astype(jnp.float32)
@@ -139,16 +538,7 @@
     block_out = (
         middle + jnp.dot(hidden, full_down, preferred_element_type=jnp.float32) + shifts[5]
     ).astype(jnp.bfloat16)
-    again = (
-        lax.all_gather(ln_gains, "fsdp", axis=1, tiled=True),
-        lax.all_gather(biases, "fsdp", axis=1, tiled=True),
-        lax.all_gather(w_qkv, "fsdp", axis=0, tiled=True),
-        lax.all_gather(w_out, "fsdp", axis=0, tiled=True),
-        lax.all_gather(w_up, "fsdp", axis=0, tiled=True),
-        lax.all_gather(bias_up, "fsdp", axis=0, tiled=True),
-        lax.all_gather(w_down, "fsdp", axis=0, tiled=True),
-    )
-    back_qkv, back_out, back_up, back_down = (again[2], again[3], again[4], again[6])
+    back_qkv, back_out, back_up, back_down = full_qkv, full_out, full_up, full_down
     grad_out = cotangent.astype(jnp.float32)
     grad_shift_down = jnp.sum(grad_out, axis=0)
     grad_down = contract_rows(hidden, cotangent)
@@ -194,16 +584,20 @@
             grad_shift_down,
         ]
     )
-    owned = (
+    small = (
         lax.psum_scatter(grad_gains, "fsdp", scatter_dimension=1, tiled=True),
         lax.psum_scatter(grad_shifts, "fsdp", scatter_dimension=1, tiled=True),
-        lax.psum_scatter(grad_qkv, "fsdp", scatter_dimension=0, tiled=True),
-        lax.psum_scatter(grad_out_proj, "fsdp", scatter_dimension=0, tiled=True),
-        lax.psum_scatter(grad_up, "fsdp", scatter_dimension=0, tiled=True),
         lax.psum_scatter(grad_bias_up, "fsdp", scatter_dimension=0, tiled=True),
-        lax.psum_scatter(grad_down, "fsdp", scatter_dimension=0, tiled=True),
-    )
-    summed = lax.psum((owned[0], owned[1], owned[2], owned[3], owned[4], owned[5], owned[6]), "dp")
+    )
+    large = [g.astype(BF16) for g in (grad_down, grad_up, grad_out_proj, grad_qkv)]
+    if fast:
+        small = lax.psum(small, "dp")
+        large = reduce_grads(*large)
+    else:
+        large = [lax.psum_scatter(g, "fsdp", scatter_dimension=0, tiled=True) for g in large]
+        small, large = lax.psum((small, large), "dp")
+    large = [g.astype(F32) for g in large]
+    summed = (small[0], small[1], large[3], large[2], large[1], small[2], large[0])
     return (
         block_out,
         d_inputs,
@@ -218,6 +612,7 @@
 
 
 def solution(mesh):
+    fast = mesh.shape["fsdp"] == 8 and mesh.shape["dp"] == 4
     placed = (
         P(("fsdp", "dp"), None),
         P(("fsdp", "dp")),
@@ -231,7 +626,7 @@
         P(("fsdp", "dp"), None),
     )
     return jax.shard_map(
-        per_device,
+        functools.partial(per_device, fast),
         mesh=mesh,
         in_specs=placed,
         out_specs=(

time: 1210 us -> 720 us (0.60)
  waiting for transfers between devices: 627 us -> 0.04 us
  Pallas kernels: 0 us -> 161 us
  local copies, waits for them, and re-layouts: 80.1 us -> 66.6 us
    reduce_scatter x4 -> x0, waiting for transfers between devices: 400 us -> none  [the longest x1 165 us: per_device(): lax.psum_scatter(grad_down, 'fsdp', scatter_dimension=0, tiled=True)]
    pallas_call x0 -> x2, Pallas kernels: none -> 161 us  [the longest x1 90 us: reduce_grads(): pl.pallas_call(reduce_kernel, out_shape=[jax.ShapeDtypeStruct(s, BF16) fo...]
    unnamed x13 -> x4, waiting for transfers between devices: 80 us -> 0.04 us
    all_gather x4 -> x0, waiting for transfers between devices: 77.7 us -> none  [the longest x1 68.6 us: per_device(): lax.all_gather(w_down, 'fsdp', axis=0, tiled=True)]
    psum x1 -> x0, waiting for transfers between devices: 69.4 us -> none  [per_device(): lax.psum((owned[0], owned[1], owned[2], owned[3], owned[4], owned[5], own...]
    unnamed x119 -> x123, local copies, waits for them, and re-layouts: 28.5 us -> 15.6 us
  transfers between devices with their start and end apart: 11 -> 2, of which waited for: 8 -> 0; matrix products, arithmetic and copies ran while one was open for 31% -> 9% of each run, Pallas kernels for 0% -> 13%
where the time goes in v1:
time: 720 us; the launch traced here: 711 us
  matrix products  249 us (35%)
  Pallas kernels  161 us (22%)
  blocking collectives  116 us (16%)
  other arithmetic  101 us (14%)
  local copies, waits for them, and re-layouts  66.6 us (9%)
  between operations  15.6 us (2%)
    pallas_call x1, Pallas kernels, reduce_grads(): pl.pallas_call(reduce_kernel, out_shape=[jax.ShapeDtypeStruct(s, BF16) fo...  90 us
    pallas_call x1, Pallas kernels, gather_weights(): pl.pallas_call(gather_kernel, out_shape=[jax.ShapeDtypeStruct((a.shape[0]...  71.5 us
    convert_element_type x2, other arithmetic, attend_backward(): d_scores = (attn_probs * (d_probs - inner)).astype(jnp.bfloat16)  42.5 us
    dot_general x4, matrix products, block_scores(): jnp.einsum('qhd,khd->hqk', split_heads(query), split_heads(keys), preferr...  41.3 us
    dot_general x4, matrix products, contract_cols(): lax.dot_general(left, right, (((1,), (1,)), ((), ())), preferred_element_...  40.2 us
    dot_general x2, matrix products, attend_backward(): jnp.einsum('qhd,khd->hqk', grad_heads, split_heads(values), preferred_ele...  36.2 us
    unnamed x1, blocking collectives  35.1 us
    dot_general x4, matrix products, contract_rows(): lax.dot_general(left, right, (((0,), (0,)), ((), ())), preferred_element_...  31.1 us
  transfers between devices with their start and end apart: 2, of which 0 were waited for; matrix products, arithmetic and copies ran while one was open for 9% of the time, Pallas kernels for 13%

profile of v1, /device:TPU:0, one launch (start us, length us, event | category | flops | bytes accessed | tf_op | source)
XLA Modules:
  0.0 711.2 jit_solution(12358833387341993741)
XLA Ops:
  8.6 22.4 %all-gather = bf16[8,96,2]{1,2,0:T(2,128)(2,1)S(1)} all-gather(bf16[1,96,2]{1,2,0:T(2,128)(2,1)} %bitcast.183), channel_id=1, replica_groups=mesh['fsdp'=8,'dp'=4] {'fsdp'}, dimensions={0}, use_global_device_ids=true | all-gather | bytes 3456 | tf_op jit(solution)/shard_map/all_gather | solution.py:492
  31.1 26.0 %all-gather.2 = bf16[8,1,384]{2,1,0:T(2,128)(2,1)S(1)} all-gather(bf16[1,1,384]{2,1,0:T(2,128)(2,1)S(1)} %reshape.253), channel_id=1, replica_groups=mesh['fsdp'=8,'dp'=4] {'fsdp'}, dimensions={0}, use_global_device_ids=true | all-gather | bytes 6912 | tf_op jit(solution)/shard_map/all_gather | solution.py:497
  57.8 26.2 %all-gather.1 = bf16[8,96,6]{1,2,0:T(8,128)(2,1)S(1)} all-gather(bf16[1,96,6]{1,2,0:T(8,128)(2,1)} %bitcast.182), channel_id=1, replica_groups=mesh['fsdp'=8,'dp'=4] {'fsdp'}, dimensions={0}, use_global_device_ids=true | all-gather | bytes 10368 | tf_op jit(solution)/shard_map/all_gather | solution.py:493
  84.1 1.8 copy.79
  87.3 1.6 copy.87
  89.6 71.5 %gather.1 = (bf16[768,2304]{1,0:T(8,128)(2,1)}, bf16[768,768]{1,0:T(8,128)(2,1)}, bf16[768,3072]{1,0:T(8,128)(2,1)}, bf16[3072,768]{1,0:T(8,128)(2,1)}) custom-call(bf16[96,2304]{1,0:T(8,128)(2,1)} %q_ref.1, bf16[96,768]{1,0:T(8,128)(2,1)} %o_ref.1, bf16[96,3072]{1,0:T(8,128)(2,1)} %u_ref.1, bf16[384,768]{1,0:T(8,128)(2,1)} %d_ref.1), custom_call_target="tpu_custom_call" | custom-call | tf_op jit(solution)/shard_map/gather/pallas_call | solution.py:296
  161.1 6.4 add_convert_fusion
  169.0 1.6 copy.84
  170.6 1.7 copy.83
  172.3 1.6 copy.82
  175.2 75.9 %while.27 = (s32[]{:T(128)}, bf16[2,512,768]{2,1,0:T(8,128)(2,1)}, f32[2,12,512]{2,1,0:T(8,128)S(1)}, s32[2,512]{1,0:T(2,128)S(1)}, s32[1024]{0:T(1024)S(1)}, /*...) while((s32[]{:T(128)}, bf16[2,512,768]{2,1,0:T(8,128)(2,1)}, ...), condition=%wide.region_5.6_spmd, body=%wide.region_2.5_spmd.sunk | while | flops 1686628352 | bytes 187926672 | solution.py:528
  177.0 10.5 %fusion.100 = (f32[12,512]{1,0:T(8,128)S(1)}, f32[12,512,1024]{2,1,0:T(8,128)}) fusion(pred[512,1024]{1,0:T(8,128)(4,1)S(1)} %broadcast_compare_fusion.4, bf16[512,12,64]{0,2,1:T(8,128)(2,1)S(1)} %bitcast.154, bf16[1024,12,64]{0,2,1:T(8,128)(2,1)S(1)} %bitcast.149), kind=kOutput, calls=%fused_computation.3.clone.1 | convolution fusion | flops 824174592 | bytes 28073984 | tf_op jit(solution)/shard_map/while/body/eval_jaxpr/qhd,khd->hqk/dot_general | solution.py:438
  187.5 12.3 %fusion.101 = f32[12,512]{1,0:T(8,128)S(1)} fusion(f32[12,512,1024]{2,1,0:T(8,128)} %get-tuple-element.468, f32[12,512]{1,0:T(8,128)S(1)} %get-tuple-element.469, pred[512,1024]{1,0:T(8,128)(4,1)S(1)} %broadcast_compare_fusion.4), kind=kLoop, calls=%fused_computation.4.clone.1 | loop fusion | flops 25159680 | bytes 25739264 | tf_op jit(solution)/shard_map/while/body/eval_jaxpr/reduce_sum | solution.py:450
  199.8 3.1 copy-done
  202.9 9.0 %fusion.102 = bf16[12,512,64]{1,2,0:T(8,128)(2,1)S(1)} fusion(bf16[1024,12,64]{0,2,1:T(8,128)(2,1)} %bitcast.127, f32[12,512,1024]{2,1,0:T(8,128)S(1)} %copy-done, f32[12,512]{1,0:T(8,128)S(1)} %fusion.101, f32[12,512]{1,0:T(8,128)S(1)} %get-tuple-element.469, pred[512,1024]{1,0:T(8,128)(4,1)S(1)} %broadcast_compare_fusion.4), kind=kOutput, calls=%fused_computation.5.clone.1 | convolution fusion | flops 836763648 | bytes 28098560 | tf_op jit(solution)/shard_map/while/body/eval_jaxpr/hqk,khd->qhd/dot_general | solution.py:452
  214.7 10.6 %fusion.100 = (f32[12,512]{1,0:T(8,128)S(1)}, f32[12,512,1024]{2,1,0:T(8,128)}) fusion(pred[512,1024]{1,0:T(8,128)(4,1)S(1)} %broadcast_compare_fusion.4, bf16[512,12,64]{0,2,1:T(8,128)(2,1)S(1)} %bitcast.154, bf16[1024,12,64]{0,2,1:T(8,128)(2,1)S(1)} %bitcast.149), kind=kOutput, calls=%fused_computation.3.clone.1 | convolution fusion | flops 824174592 | bytes 28073984 | tf_op jit(solution)/shard_map/while/body/eval_jaxpr/qhd,khd->hqk/dot_general | solution.py:438
  225.3 12.3 %fusion.101 = f32[12,512]{1,0:T(8,128)S(1)} fusion(f32[12,512,1024]{2,1,0:T(8,128)} %get-tuple-element.468, f32[12,512]{1,0:T(8,128)S(1)} %get-tuple-element.469, pred[512,1024]{1,0:T(8,128)(4,1)S(1)} %broadcast_compare_fusion.4), kind=kLoop, calls=%fused_computation.4.clone.1 | loop fusion | flops 25159680 | bytes 25739264 | tf_op jit(solution)/shard_map/while/body/eval_jaxpr/reduce_sum | solution.py:450
  237.6 3.1 copy-done
  240.7 9.0 %fusion.102 = bf16[12,512,64]{1,2,0:T(8,128)(2,1)S(1)} fusion(bf16[1024,12,64]{0,2,1:T(8,128)(2,1)} %bitcast.127, f32[12,512,1024]{2,1,0:T(8,128)S(1)} %copy-done, f32[12,512]{1,0:T(8,128)S(1)} %fusion.101, f32[12,512]{1,0:T(8,128)S(1)} %get-tuple-element.469, pred[512,1024]{1,0:T(8,128)(4,1)S(1)} %broadcast_compare_fusion.4), kind=kOutput, calls=%fused_computation.5.clone.1 | convolution fusion | flops 836763648 | bytes 28098560 | tf_op jit(solution)/shard_map/while/body/eval_jaxpr/hqk,khd->qhd/dot_general | solution.py:452
  251.2 4.0 fusion.47
  256.0 5.6 fusion.44
  261.6 19.2 %convert_reduce_fusion = (f32[3072]{0:T(1024)}, bf16[1024,3072]{1,0:T(8,128)(2,1)}) fusion(f32[1024,3072]{1,0:T(8,128)S(1)} %fusion.44, f32[3072]{0:T(1024)S(1)} %bitcast.179, bf16[3072,768]{1,0:T(8,128)(2,1)} %get-tuple-element.123, bf16[1024,768]{1,0:T(8,128)(2,1)S(1)} %copy-done.24), kind=kOutput, calls=%fused_computation.47 | convolution fusion | flops 4916769792 | bytes 25190400 | tf_op jit(solution)/shard_map/dot_general | solution.py:428
  280.8 9.5 %fusion.49 = (f32[768]{0:T(1024)}, f32[1024,768]{1,0:T(8,128)}) fusion(bf16[1024,3072]{1,0:T(8,128)(2,1)} %get-tuple-element.354, bf16[768,3072]{1,0:T(8,128)(2,1)S(1)} %bitcast.164), kind=kOutput, calls=%fused_computation.116 | convolution fusion | flops 4832623616 | bytes 14158848 | tf_op jit(solution)/shard_map/dot_general | solution.py:428
  290.3 3.5 copy.88
  293.8 3.9 multiply_reduce_fusion.1
  301.7 2.6 convolution_convert_fusion.3
  305.6 178.8 %while.28 = (s32[]{:T(128)}, f32[1024,768]{0,1:T(8,128)}, f32[1024,768]{0,1:T(8,128)}, bf16[2,512,768]{2,1,0:T(8,128)(2,1)}, bf16[2,512,768]{1,2,0:T(8,128)(2,1)...) while((s32[]{:T(128)}, f32[1024,768]{0,1:T(8,128)}, ...), condition=%wide.region_12.13_spmd.clone, body=%wide.region_10.12_spmd.clone.sunk | while | flops 4126140416 | bytes 298764608 | solution.py:565
  309.7 10.1 %fusion.113 = f32[12,512,1024]{2,1,0:T(8,128)} fusion(bf16[512,12,64]{0,2,1:T(8,128)(2,1)S(1)} %bitcast.152, bf16[1024,12,64]{0,2,1:T(8,128)(2,1)S(1)} %bitcast.150), kind=kOutput, calls=%fused_computation.117.clone.1 | convolution fusion | flops 805306368 | bytes 27525120 | tf_op jit(solution)/shard_map/while/body/eval_jaxpr/qhd,khd->hqk/dot_general | solution.py:438
  319.8 13.0 %fusion.114 = f32[12,64,1024]{2,1,0:T(8,128)} fusion(bf16[512,12,64]{0,2,1:T(8,128)(2,1)S(1)} %bitcast.156, f32[12,512,1024]{2,1,0:T(8,128)} %fusion.113, f32[12,512]{1,0:T(8,128)S(1)} %dynamic-slice_bitcast_fusion.2, pred[512,1024]{1,0:T(8,128)(4,1)S(1)} %broadcast_compare_fusion.5), kind=kOutput, calls=%fused_computation.17.clone.1 | convolution fusion | flops 830472192 | bytes 29646848 | tf_op jit(solution)/shard_map/while/body/eval_jaxpr/hqk,qhd->khd/dot_general | solution.py:463
  332.8 18.1 %multiply_reduce_fusion.5 = (f32[12,512]{1,0:T(8,128)S(1)}, f32[12,512,1024]{2,1,0:T(8,128)}) fusion(f32[12,512,1024]{2,1,0:T(8,128)} %fusion.113, f32[12,512]{1,0:T(8,128)S(1)} %dynamic-slice_bitcast_fusion.2, pred[512,1024]{1,0:T(8,128)(4,1)S(1)} %broadcast_compare_fusion.5, bf16[512,12,64]{0,2,1:T(8,128)(2,1)} %bitcast.155, ...), kind=kOutput, calls=%fused_computation.14.clone.1 | convolution fusion | flops 836757504 | bytes 53264384 | tf_op jit(solution)/shard_map/while/body/eval_jaxpr/qhd,khd->hqk/dot_general | solution.py:464
  350.9 21.2 %multiply_convert_fusion.5 = bf16[12,512,1024]{2,1,0:T(8,128)(2,1)} fusion(f32[12,512,1024]{2,1,0:T(8,128)} %get-tuple-element.481, f32[12,512,1024]{2,1,0:T(8,128)} %fusion.113, f32[12,512]{1,0:T(8,128)S(1)} %get-tuple-element.482, f32[12,512]{1,0:T(8,128)S(1)} %dynamic-slice_bitcast_fusion.2, pred[512,1024]{1,0:T(8,128)(4,1)S(1)} %broadcast_compare_fusion.5), kind=kLoop, calls=%fused_computation.13.clone.1 | loop fusion | flops 37748736 | bytes 63488000 | tf_op jit(solution)/shard_map/while/body/eval_jaxpr/convert_element_type | solution.py:468
  372.1 8.5 %convolution_multiply_fusion.5 = bf16[12,512,64]{1,2,0:T(8,128)(2,1)S(1)} fusion(bf16[12,512,1024]{2,1,0:T(8,128)(2,1)} %multiply_convert_fusion.5, bf16[1024,12,64]{0,2,1:T(8,128)(2,1)S(1)} %bitcast.151), kind=kOutput, calls=%fused_computation.22.clone.1 | convolution fusion | flops 806092800 | bytes 14942208 | tf_op jit(solution)/shard_map/while/body/eval_jaxpr/hqk,khd->qhd/dot_general | solution.py:471
  380.6 7.0 convolution_multiply_fusion.4
  387.9 2.3 bitcast_add_fusion.3
  390.3 1.7 copy-done.2
  392.0 1.6 copy-done.5
  398.8 10.1 %fusion.113 = f32[12,512,1024]{2,1,0:T(8,128)} fusion(bf16[512,12,64]{0,2,1:T(8,128)(2,1)S(1)} %bitcast.152, bf16[1024,12,64]{0,2,1:T(8,128)(2,1)S(1)} %bitcast.150), kind=kOutput, calls=%fused_computation.117.clone.1 | convolution fusion | flops 805306368 | bytes 27525120 | tf_op jit(solution)/shard_map/while/body/eval_jaxpr/qhd,khd->hqk/dot_general | solution.py:438
  408.9 13.0 %fusion.114 = f32[12,64,1024]{2,1,0:T(8,128)} fusion(bf16[512,12,64]{0,2,1:T(8,128)(2,1)S(1)} %bitcast.156, f32[12,512,1024]{2,1,0:T(8,128)} %fusion.113, f32[12,512]{1,0:T(8,128)S(1)} %dynamic-slice_bitcast_fusion.2, pred[512,1024]{1,0:T(8,128)(4,1)S(1)} %broadcast_compare_fusion.5), kind=kOutput, calls=%fused_computation.17.clone.1 | convolution fusion | flops 830472192 | bytes 29646848 | tf_op jit(solution)/shard_map/while/body/eval_jaxpr/hqk,qhd->khd/dot_general | solution.py:463
  421.9 18.1 %multiply_reduce_fusion.5 = (f32[12,512]{1,0:T(8,128)S(1)}, f32[12,512,1024]{2,1,0:T(8,128)}) fusion(f32[12,512,1024]{2,1,0:T(8,128)} %fusion.113, f32[12,512]{1,0:T(8,128)S(1)} %dynamic-slice_bitcast_fusion.2, pred[512,1024]{1,0:T(8,128)(4,1)S(1)} %broadcast_compare_fusion.5, bf16[512,12,64]{0,2,1:T(8,128)(2,1)} %bitcast.155, ...), kind=kOutput, calls=%fused_computation.14.clone.1 | convolution fusion | flops 836757504 | bytes 53264384 | tf_op jit(solution)/shard_map/while/body/eval_jaxpr/qhd,khd->hqk/dot_general | solution.py:464
  440.0 21.2 %multiply_convert_fusion.5 = bf16[12,512,1024]{2,1,0:T(8,128)(2,1)} fusion(f32[12,512,1024]{2,1,0:T(8,128)} %get-tuple-element.481, f32[12,512,1024]{2,1,0:T(8,128)} %fusion.113, f32[12,512]{1,0:T(8,128)S(1)} %get-tuple-element.482, f32[12,512]{1,0:T(8,128)S(1)} %dynamic-slice_bitcast_fusion.2, pred[512,1024]{1,0:T(8,128)(4,1)S(1)} %broadcast_compare_fusion.5), kind=kLoop, calls=%fused_computation.13.clone.1 | loop fusion | flops 37748736 | bytes 63488000 | tf_op jit(solution)/shard_map/while/body/eval_jaxpr/convert_element_type | solution.py:468
  461.2 8.5 %convolution_multiply_fusion.5 = bf16[12,512,64]{1,2,0:T(8,128)(2,1)S(1)} fusion(bf16[12,512,1024]{2,1,0:T(8,128)(2,1)} %multiply_convert_fusion.5, bf16[1024,12,64]{0,2,1:T(8,128)(2,1)S(1)} %bitcast.151), kind=kOutput, calls=%fused_computation.22.clone.1 | convolution fusion | flops 806092800 | bytes 14942208 | tf_op jit(solution)/shard_map/while/body/eval_jaxpr/hqk,khd->qhd/dot_general | solution.py:471
  469.7 7.0 convolution_multiply_fusion.4
  477.0 2.3 bitcast_add_fusion.3
  479.4 1.7 copy-done.2
  484.3 3.2 copy.94
  487.5 1.7 copy.95
  489.2 8.9 %fusion.48 = (f32[768]{0:T(1024)S(1)}, f32[1024,768]{1,0:T(8,128)}) fusion(bf16[768,2304]{1,0:T(8,128)(2,1)} %get-tuple-element.119, bf16[1024,768]{1,0:T(8,128)(2,1)} %copy.95, bf16[1024,768]{1,0:T(8,128)(2,1)} %copy.94, bf16[1024,768]{1,0:T(8,128)(2,1)} %bitcast.160), kind=kOutput, calls=%fused_computation.115 | convolution fusion | flops 3638820096 | bytes 11406336 | tf_op jit(solution)/shard_map/dot_general | solution.py:428
  498.1 3.7 copy.96
  501.9 2.6 fusion.32
  507.1 1.7 convert_reduce_fusion.4
  508.9 6.5 convert_reduce_fusion.2
  516.8 12.8 %convolution_convert_fusion.1 = bf16[3072,768]{1,0:T(8,128)(2,1)} fusion(bf16[1024,768]{1,0:T(8,128)(2,1)} %param.23, f32[1024,3072]{1,0:T(8,128)} %copy-done.18, f32[3072]{0:T(1024)S(1)} %bitcast.180), kind=kOutput, calls=%fused_computation.51 | convolution fusion | flops 4865654784 | bytes 18886656 | tf_op jit(solution)/shard_map/dot_general | solution.py:422
  529.7 10.1 %convolution_convert_fusion = bf16[768,3072]{1,0:T(8,128)(2,1)} fusion(bf16[1024,3072]{1,0:T(8,128)(2,1)} %get-tuple-element.354, f32[1024,768]{0,1:T(8,128)S(1)} %copy-done.12, f32[768]{0:T(1024)S(1)} %copy-done.37, f32[768]{0:T(1024)S(1)} %copy-done.33, f32[1024]{0:T(1024)S(1)} %copy-done.35, f32[1024]{0:T(1024)S(1)} %copy-done.30), kind=kOutput, calls=%fused_computation.50 | convolution fusion | flops 4838129664 | bytes 14170112 | tf_op jit(solution)/shard_map/dot_general | solution.py:422
  539.8 5.9 convolution_convert_fusion.2
  545.7 9.6 %add_convert_fusion.1 = bf16[1024,768]{0,1:T(8,128)(2,1)S(1)} fusion(f32[1024,768]{0,1:T(8,128)S(1)} %copy-done.12, bf16[3072,768]{1,0:T(8,128)(2,1)S(1)} %bitcast.185, f32[768]{0:T(1024)S(1)} %copy-done.52, f32[1024,3072]{1,0:T(8,128)} %copy-done.18, f32[3072]{0:T(1024)S(1)} %bitcast.181), kind=kOutput, calls=%fused_computation.78 | convolution fusion | flops 4865654784 | bytes 22035456 | tf_op jit(solution)/shard_map/dot_general | solution.py:539
  555.3 2.4 convolution_convert_fusion.4
  559.3 90.0 %reduce.17 = (bf16[384,768]{1,0:T(8,128)(2,1)}, bf16[96,3072]{1,0:T(8,128)(2,1)}, bf16[96,768]{1,0:T(8,128)(2,1)}, bf16[96,2304]{1,0:T(8,128)(2,1)}) custom-call(bf16[4,2,6,64,768]{4,3,2,1,0:T(8,128)(2,1)} %bitcast.165, bf16[4,2,96,3072]{3,2,1,0:T(8,128)(2,1)} %bitcast.166, bf16[4,2,96,768]{3,2,1,0:T(8,128)(2,1)} %bitcast.172, bf16[4,2,96,2304]{3,2,1,0:T(8,128)(2,1)} %bitcast.167), custom_call_target="tpu_custom_call" | custom-call | tf_op jit(solution)/shard_map/reduce/pallas_call | solution.py:377
  649.3 1.8 convert_element_type.110
  651.1 2.0 convert_element_type.109
  653.1 2.2 convert_element_type.111
  655.3 2.2 convert_element_type.113
  657.4 2.4 copy.100
  661.0 35.1 %all-reduce = f32[3072]{0:T(1024)S(1)} all-reduce(f32[3072]{0:T(1024)S(1)} %copy-done.50), channel_id=4, replica_groups=mesh['fsdp'=8,'dp'=4] {'fsdp'}, use_global_device_ids=true, to_apply=%region_28.29.clone | all-reduce | flops 3072 | bytes 24576
  697.9 6.3 all-reduce.1
  (219 shorter events, 38.9 us)
Async XLA Ops:
  7.2 689.0 %reduce-scatter.7.cloned.1.call-start = ((), (), s32[]{:S(2)}) async-start(), calls=%async_computation.2 | async-start | bytes 442368
  84.1 3.2 copy-start.23
  85.9 75.1 %copy-start.8 = (bf16[1024,768]{0,1:T(8,128)(2,1)}, bf16[1024,768]{0,1:T(8,128)(2,1)S(1)}, u32[]{:S(2)}) copy-start(bf16[1024,768]{0,1:T(8,128)(2,1)S(1)} %copy.79) | copy-start | bytes 4718596
  86.2 74.9 %copy-start.38 = (f32[1024]{0:T(1024)}, f32[1024]{0:T(1024)S(1)}, u32[]{:S(2)}) copy-start(f32[1024]{0:T(1024)S(1)} %broadcast_multiply_fusion.1) | copy-start | bytes 12292
  87.3 80.2 %copy-start.42 = (f32[1024]{0:T(1024)}, f32[1024]{0:T(1024)S(1)}, u32[]{:S(2)}) copy-start(f32[1024]{0:T(1024)S(1)} %fusion.38) | copy-start | bytes 12292
  89.6 77.9 %copy-start.40 = (f32[768]{0:T(1024)}, f32[768]{0:T(1024)S(1)}, u32[]{:S(2)}) copy-start(f32[768]{0:T(1024)S(1)} %get-tuple-element.355) | copy-start | bytes 9220
  89.6 77.9 %copy-start.53 = (f32[768]{0:T(1024)}, f32[768]{0:T(1024)S(1)}, u32[]{:S(2)}) copy-start(f32[768]{0:T(1024)S(1)} %get-tuple-element.291) | copy-start | bytes 9220
  172.3 2.9 copy-start.31
  175.2 76.0 %copy-start.55 = (f32[768]{0:T(1024)S(1)}, f32[768]{0:T(1024)}, u32[]{:S(2)}) copy-start(f32[768]{0:T(1024)} %get-tuple-element.288) | copy-start | bytes 9220
  187.5 15.4 %copy-start = (f32[12,512,1024]{2,1,0:T(8,128)S(1)}, f32[12,512,1024]{2,1,0:T(8,128)}, u32[]{:S(2)}) copy-start(f32[12,512,1024]{2,1,0:T(8,128)} %get-tuple-element.468) | copy-start | bytes 75497472 | tf_op jit(solution)/shard_map/while
  225.3 15.4 %copy-start = (f32[12,512,1024]{2,1,0:T(8,128)S(1)}, f32[12,512,1024]{2,1,0:T(8,128)}, u32[]{:S(2)}) copy-start(f32[12,512,1024]{2,1,0:T(8,128)} %get-tuple-element.468) | copy-start | bytes 75497472 | tf_op jit(solution)/shard_map/while
  251.2 4.5 slice-start
  251.2 4.5 slice-start.1
  255.2 6.4 copy-start.10
  255.3 43.1 %copy-start.29 = (f32[1024]{0:T(1024)}, f32[1024]{0:T(1024)S(1)}, u32[]{:S(2)}) copy-start(f32[1024]{0:T(1024)S(1)} %broadcast_multiply_fusion) | copy-start | bytes 12292
  255.7 42.7 %copy-start.34 = (f32[1024]{0:T(1024)}, f32[1024]{0:T(1024)S(1)}, u32[]{:S(2)}) copy-start(f32[1024]{0:T(1024)S(1)} %fusion.39) | copy-start | bytes 12292
  256.0 5.6 copy-start.24
  256.0 5.6 copy-start.48
  261.6 19.2 %copy-start.18 = (f32[1024,3072]{1,0:T(8,128)}, f32[1024,3072]{1,0:T(8,128)S(1)}, u32[]{:S(2)}) copy-start(f32[1024,3072]{1,0:T(8,128)S(1)} %fusion.44) | copy-start | bytes 37748740
  293.8 4.5 copy-start.11
  293.8 4.7 copy-start.15
  299.3 1.7 copy-start.14
  299.9 1.8 copy-start.57
  301.7 2.6 copy-start.26
  309.7 10.1 %copy-start.7 = (bf16[1,512,768]{1,2,0:T(8,128)(2,1)S(1)}, bf16[1,512,768]{1,2,0:T(8,128)(2,1)}, u32[]{:S(2)}) copy-start(bf16[1,512,768]{1,2,0:T(8,128)(2,1)} %copy.134) | copy-start | bytes 2359300 | tf_op jit(solution)/shard_map/while
  380.6 7.1 copy-start.1
  380.6 7.1 copy-start.4
  380.6 7.3 %copy-start.6 = (f32[12,64,1024]{2,1,0:T(8,128)S(1)}, f32[12,64,1024]{2,1,0:T(8,128)}, u32[]{:S(2)}) copy-start(f32[12,64,1024]{2,1,0:T(8,128)} %fusion.114) | copy-start | bytes 9437188 | tf_op jit(solution)/shard_map/while
  390.2 1.7 copy-start.2
  398.8 10.1 %copy-start.7 = (bf16[1,512,768]{1,2,0:T(8,128)(2,1)S(1)}, bf16[1,512,768]{1,2,0:T(8,128)(2,1)}, u32[]{:S(2)}) copy-start(bf16[1,512,768]{1,2,0:T(8,128)(2,1)} %copy.134) | copy-start | bytes 2359300 | tf_op jit(solution)/shard_map/while
  469.7 7.1 copy-start.1
  469.7 7.1 copy-start.4
  469.7 7.3 %copy-start.6 = (f32[12,64,1024]{2,1,0:T(8,128)S(1)}, f32[12,64,1024]{2,1,0:T(8,128)}, u32[]{:S(2)}) copy-start(f32[12,64,1024]{2,1,0:T(8,128)} %fusion.114) | copy-start | bytes 9437188 | tf_op jit(solution)/shard_map/while
  479.3 1.7 copy-start.2
  484.3 3.2 copy-start.3
  498.1 3.7 copy-start.9
  498.1 3.7 copy-start.39
  498.1 3.7 copy-start.41
  501.9 2.6 copy-start.45
  501.9 2.8 copy-start.13
  501.9 2.8 copy-start.43
  504.7 4.1 copy-start.17
  504.7 4.1 copy-start.47
  507.1 189.9 %reduce-scatter.9.cloned.1.call-start = ((), (), s32[]{:S(2)}) async-start(), calls=%async_computation.3 | async-start | bytes 442368
  508.8 6.5 copy-start.21
  508.9 6.8 copy-start.56
  508.9 7.9 %copy-start.49 = (f32[8,1,384]{2,1,0:T(1,128)S(1)}, f32[8,1,384]{2,1,0:T(1,128)}, u32[]{:S(2)}) copy-start(f32[8,1,384]{2,1,0:T(1,128)} %convert_element_type.116) | copy-start | bytes 36868
  516.8 12.8 %copy-start.12 = (f32[1024,768]{0,1:T(8,128)S(1)}, f32[1024,768]{0,1:T(8,128)}, u32[]{:S(2)}) copy-start(f32[1024,768]{0,1:T(8,128)} %copy-done.10) | copy-start | bytes 9437188
  516.8 12.8 %copy-start.30 = (f32[1024]{0:T(1024)S(1)}, f32[1024]{0:T(1024)}, u32[]{:S(2)}) copy-start(f32[1024]{0:T(1024)} %copy-done.29) | copy-start | bytes 12292
  516.8 12.8 %copy-start.33 = (f32[768]{0:T(1024)S(1)}, f32[768]{0:T(1024)}, u32[]{:S(2)}) copy-start(f32[768]{0:T(1024)} %get-tuple-element.356) | copy-start | bytes 9220
  516.8 12.8 %copy-start.35 = (f32[1024]{0:T(1024)S(1)}, f32[1024]{0:T(1024)}, u32[]{:S(2)}) copy-start(f32[1024]{0:T(1024)} %copy-done.34) | copy-start | bytes 12292
  516.8 12.8 %copy-start.37 = (f32[768]{0:T(1024)S(1)}, f32[768]{0:T(1024)}, u32[]{:S(2)}) copy-start(f32[768]{0:T(1024)} %get-tuple-element.286) | copy-start | bytes 9220
  529.6 10.1 %copy-start.20 = (bf16[2,512,768]{2,1,0:T(8,128)(2,1)S(1)}, bf16[2,512,768]{2,1,0:T(8,128)(2,1)}, u32[]{:S(2)}) copy-start(bf16[2,512,768]{2,1,0:T(8,128)(2,1)} %get-tuple-element.125) | copy-start | bytes 4718596
  529.6 10.1 %copy-start.22 = (bf16[1024,768]{1,0:T(8,128)(2,1)S(1)}, bf16[1024,768]{1,0:T(8,128)(2,1)}, u32[]{:S(2)}) copy-start(bf16[1024,768]{1,0:T(8,128)(2,1)} %copy.95) | copy-start | bytes 4718596
  529.6 10.1 %copy-start.28 = (bf16[1024,768]{1,0:T(8,128)(2,1)S(1)}, bf16[1024,768]{1,0:T(8,128)(2,1)}, u32[]{:S(2)}) copy-start(bf16[1024,768]{1,0:T(8,128)(2,1)} %copy.94) | copy-start | bytes 4718596
  529.6 10.1 %copy-start.54 = (f32[768]{0:T(1024)S(1)}, f32[768]{0:T(1024)}, u32[]{:S(2)}) copy-start(f32[768]{0:T(1024)} %copy-done.53) | copy-start | bytes 9220
  529.6 16.0 %slice-start.2 = ((s8[4718592]{0:T(1024)(128)(4,1)}), s8[524288]{0:T(1024)(128)(4,1)S(1)}, s32[]{:S(2)}) async-start(s8[4718592]{0:T(1024)(128)(4,1)} %bitcast.184), calls=%async_computation.6 | async-start | bytes 1048576
  539.7 5.9 copy-start.52
  539.7 5.9 slice-start.3
  545.6 9.7 %copy-start.25 = (bf16[2,512,768]{2,1,0:T(8,128)(2,1)S(1)}, bf16[2,512,768]{2,1,0:T(8,128)(2,1)}, u32[]{:S(2)}) copy-start(bf16[2,512,768]{2,1,0:T(8,128)(2,1)} %get-tuple-element.120) | copy-start | bytes 4718596
  545.7 9.7 %copy-start.27 = (bf16[1024,768]{0,1:T(8,128)(2,1)S(1)}, bf16[1024,768]{0,1:T(8,128)(2,1)}, u32[]{:S(2)}) copy-start(bf16[1024,768]{0,1:T(8,128)(2,1)} %copy-done.26) | copy-start | bytes 4718596
  649.3 8.1 %copy-start.19 = (f32[1024,768]{0,1:T(8,128)S(1)}, f32[1024,768]{0,1:T(8,128)}, u32[]{:S(2)}) copy-start(f32[1024,768]{0,1:T(8,128)} %get-tuple-element.343) | copy-start | bytes 9437188
  657.4 2.4 copy-start.58
  657.4 3.6 copy-start.50
  (8 other events, 10.0 us)
Sparse Core Ops, SparseCore 0:
  507.2 62.4 reduce-scatter.6
  573.0 63.6 reduce-scatter.8
